TPU v7x, 32 devices: a whole 2x2x4 slice. The times are simulated.
32 devices in a mesh: row: 4 (over z), col: 8 (over y, x, core).
Axes of the slice: x: 2, y: 2, z: 4, core: 2. Of those that a mesh axis runs over, the one named last changes fastest.
Arguments:
- tokens: bfloat16 [2048, 2048], P(('row', 'col')), may hold values from -6 to 6
- timestep: int32 [1], replicated, may hold values from 0 to 999
- mod_weight: float32 [256, 2048], replicated, may hold values from -0.375 to 0.375
- qkv_weight: bfloat16 [3, 2048, 2048], P(None, None, 'col'), may hold values from -0.125 to 0.125
- attn_scale: float32 [16], P('col'), may hold values from 4 to 40
- out_weight: bfloat16 [2048, 2048], P('col'), may hold values from -0.5 to 0.5
- grad_update: bfloat16 [2048, 2048], P(('row', 'col')), may hold values from -6 to 6
Outputs:
- update: bfloat16 [2048, 2048], P(('row', 'col'))
- grad_tokens: bfloat16 [2048, 2048], P(('row', 'col'))
- grad_qkv: float32 [3, 2048, 2048], P(None, 'row', 'col')
- grad_out: float32 [2048, 2048], P('col', 'row')
All inputs are finite; a program needn't handle non-finite values.
Results may differ from a plain program's by a relative error of at most 0.018.
Values may be sent and summed in bfloat16 or wider, within the bound.
A program may use at most 128 MiB of HBM per device.

v0:
```python
import math
import jax
import jax.numpy as jnp
from jax import lax
from jax.sharding import PartitionSpec as P

epsilon = 1e-06


def embed(timestep, count):
    index = jnp.arange(count, dtype=jnp.float32)
    freqs = jnp.exp(-math.log(10000.0) * index / count)
    angles = timestep.astype(jnp.float32)[0] * freqs
    return jnp.concatenate([jnp.cos(angles), jnp.sin(angles)])


def unit_rows(values):
    factor = lax.rsqrt(jnp.mean(values * values, -1, keepdims=True) + epsilon)
    return (values * factor, factor)


def unit_grad(grad_unit, unit, factor):
    return factor * (grad_unit - unit * jnp.mean(grad_unit * unit, -1, keepdims=True))


def split_blocks(array, size):
    return array.reshape((array.shape[0] // size, size) + array.shape[1:])


def per_device(tokens, timestep, mod_weight, qkv_weight, attn_scale, out_weight, grad_update):
    tok_dev, width = tokens.shape
    heads_here = attn_scale.shape[0]
    inner = qkv_weight.shape[2]
    head_dim = inner // heads_here
    span = tok_dev * lax.axis_size("col")
    coeff = attn_scale / head_dim
    embedded = embed(timestep, mod_weight.shape[0] // 2)
    gain = 1.0 + jnp.sum(embedded[:, None] * mod_weight, 0)
    tok_float = tokens.astype(jnp.float32)
    rstd = lax.rsqrt(jnp.mean(tok_float * tok_float, -1, keepdims=True) + epsilon)
    normed = tok_float * rstd
    hidden = (normed * gain).astype(jnp.bfloat16)
    group = lax.all_gather(hidden, "col", axis=0, tiled=True)
    raw = jnp.einsum("sd,kdh->ksh", group, qkv_weight, preferred_element_type=jnp.float32)
    query_unit, query_factor = unit_rows(raw[0].reshape(span, heads_here, head_dim))
    key_unit, key_factor = unit_rows(raw[1].reshape(span, heads_here, head_dim))
    queries = query_unit.astype(jnp.bfloat16)
    key_heads = key_unit.astype(jnp.bfloat16)
    value_heads = raw[2].astype(jnp.bfloat16).reshape(span, heads_here, head_dim)
    start_state = (
        jnp.zeros((heads_here, span), jnp.float32),
        jnp.zeros((span, heads_here, head_dim), jnp.float32),
    )
    carry = start_state
    key_piece = lax.all_gather(key_heads, "row", axis=0, tiled=True)
    value_piece = lax.all_gather(value_heads, "row", axis=0, tiled=True)
    size = math.gcd(key_piece.shape[0], 512)

    def attend_step(state, block):
        key_block, value_block = block
        scores = (
            jnp.einsum("qhd,khd->hqk", queries, key_block, preferred_element_type=jnp.float32)
            * coeff[:, None, None]
        )
        weights = jnp.exp(scores - attn_scale[:, None, None])
        totals = state[0] + jnp.sum(weights, -1)
        mixed = state[1] + jnp.einsum(
            "hqk,khd->qhd",
            weights.astype(jnp.bfloat16),
            value_block,
            preferred_element_type=jnp.float32,
        )
        return ((totals, mixed), None)

    carry, unused = lax.scan(
        attend_step, carry, (split_blocks(key_piece, size), split_blocks(value_piece, size))
    )
    totals, mixed = carry
    attended_heads = (mixed / totals.T[:, :, None]).astype(jnp.bfloat16)
    attended = attended_heads.reshape(span, inner)
    rows = attended
    update = lax.psum_scatter(
        jnp.dot(rows, out_weight, preferred_element_type=jnp.float32).astype(jnp.bfloat16),
        "col",
        scatter_dimension=0,
        tiled=True,
    )
    grad_group = lax.all_gather(grad_update, "col", axis=0, tiled=True)
    out_part = lax.dot_general(
        attended, grad_group, (((0,), (0,)), ((), ())), preferred_element_type=jnp.float32
    )
    grad_out = lax.psum_scatter(
        out_part.astype(jnp.bfloat16), "row", scatter_dimension=1, tiled=True
    ).astype(jnp.float32)
    grad_attended = lax.dot_general(
        grad_group, out_weight, (((1,), (1,)), ((), ())), preferred_element_type=jnp.float32
    ).astype(jnp.bfloat16)
    grad_heads = grad_attended.reshape(span, heads_here, head_dim)
    delta = jnp.sum(grad_heads.astype(jnp.float32) * attended_heads.astype(jnp.float32), -1)
    inverse = 1.0 / totals

    def pair_terms(query_rows, grad_rows, inverse_rows, delta_rows, key_block, value_block):
        scores = (
            jnp.einsum("qhd,khd->hqk", query_rows, key_block, preferred_element_type=jnp.float32)
            * coeff[:, None, None]
        )
        probs = jnp.exp(scores - attn_scale[:, None, None]) * inverse_rows[:, :, None]
        dprobs = jnp.einsum(
            "qhd,khd->hqk", grad_rows, value_block, preferred_element_type=jnp.float32
        )
        dscores = (probs * (dprobs - delta_rows[:, :, None]) * coeff[:, None, None]).astype(
            jnp.bfloat16
        )
        return (probs, dscores)

    empty_own = jnp.zeros((span, heads_here, head_dim), jnp.float32)
    carry = empty_own
    key_piece = lax.all_gather(key_heads, "row", axis=0, tiled=True)
    value_piece = lax.all_gather(value_heads, "row", axis=0, tiled=True)
    size = math.gcd(key_piece.shape[0], 512)

    def query_step(state, block):
        key_block, value_block = block
        probs, dscores = pair_terms(queries, grad_heads, inverse, delta.T, key_block, value_block)
        return (
            state
            + jnp.einsum("hqk,khd->qhd", dscores, key_block, preferred_element_type=jnp.float32),
            None,
        )

    carry, unused = lax.scan(
        query_step, carry, (split_blocks(key_piece, size), split_blocks(value_piece, size))
    )
    grad_query = carry
    all_inverse, all_delta = (
        lax.all_gather(inverse.T, "row", axis=0, tiled=True),
        lax.all_gather(delta, "row", axis=0, tiled=True),
    )
    carry = (empty_own, empty_own)
    query_piece = lax.all_gather(queries, "row", axis=0, tiled=True)
    grad_piece = lax.all_gather(grad_heads, "row", axis=0, tiled=True)
    count = query_piece.shape[0]
    size = math.gcd(count, 512)

    def key_step(state, block):
        query_block, grad_block, inverse_block, delta_block = block
        probs, dscores = pair_terms(
            query_block, grad_block, inverse_block.T, delta_block.T, key_heads, value_heads
        )
        grad_key = state[0] + jnp.einsum(
            "hqk,qhd->khd", dscores, query_block, preferred_element_type=jnp.float32
        )
        grad_value = state[1] + jnp.einsum(
            "hqk,qhd->khd",
            probs.astype(jnp.bfloat16),
            grad_block,
            preferred_element_type=jnp.float32,
        )
        return ((grad_key, grad_value), None)

    carry, unused = lax.scan(
        key_step,
        carry,
        (
            split_blocks(query_piece, size),
            split_blocks(grad_piece, size),
            split_blocks(all_inverse, size),
            split_blocks(all_delta, size),
        ),
    )
    grad_key, grad_value = carry
    grad_q = (
        unit_grad(grad_query, query_unit, query_factor).astype(jnp.bfloat16).reshape(span, inner)
    )
    grad_k = unit_grad(grad_key, key_unit, key_factor).astype(jnp.bfloat16).reshape(span, inner)
    grad_v = grad_value.astype(jnp.bfloat16).reshape(span, inner)
    grad_raw = jnp.stack([grad_q, grad_k, grad_v])
    qkv_part = jnp.einsum("sd,ksh->kdh", group, grad_raw, preferred_element_type=jnp.float32)
    grad_qkv = lax.psum_scatter(
        qkv_part.astype(jnp.bfloat16), "row", scatter_dimension=1, tiled=True
    ).astype(jnp.float32)
    rows = grad_raw
    grad_hidden = lax.psum_scatter(
        jnp.einsum("ksh,kdh->sd", rows, qkv_weight, preferred_element_type=jnp.float32).astype(
            jnp.bfloat16
        ),
        "col",
        scatter_dimension=0,
        tiled=True,
    ).astype(jnp.float32)
    grad_normed = grad_hidden * gain
    grad_tokens = (
        rstd * (grad_normed - normed * jnp.mean(grad_normed * normed, -1, keepdims=True))
    ).astype(jnp.bfloat16)
    return (update, grad_tokens, grad_qkv, grad_out)


def solution(mesh):
    placed = (
        P(("row", "col"), None),
        P(),
        P(),
        P(None, None, "col"),
        P("col"),
        P("col", None),
        P(("row", "col"), None),
    )
    return jax.shard_map(
        per_device,
        mesh=mesh,
        in_specs=placed,
        out_specs=(
            P(("row", "col"), None),
            P(("row", "col"), None),
            P(None, "row", "col"),
            P("col", "row"),
        ),
        check_vma=False,
    )
```

profile of v0, /device:TPU:0, one launch (start us, length us, event | category | flops | bytes accessed | tf_op | source)
XLA Modules:
  0.0 422.1 jit_solution(2159010349905390229)
XLA Ops:
  8.1 1.9 multiply_reduce_fusion
  11.1 30.6 %all-gather.7.cloned.1.call-done = bf16[512,2048]{1,0:T(8,128)(2,1)} async-done(((bf16[64,2048]{1,0:T(8,128)(2,1)}), bf16[512,2048]{1,0:T(8,128)(2,1)}) %all-gather.7.cloned.1.call-update) | async-done | bytes 2097168 | tf_op jit(solution)/shard_map/all_gather | solution.py:43
  41.7 3.4 fusion.54
  48.8 1.8 slice.17
  51.3 1.8 copy.43
  53.1 1.8 copy.45
  54.9 2.0 copy.31
  60.4 16.5 %all-gather.9.cloned.1.call-done = bf16[2048,2,128]{0,2,1:T(8,128)(2,1)} async-done(((bf16[512,2,128]{0,2,1:T(8,128)(2,1)}), bf16[2048,2,128]{0,2,1:T(8,128)(2,1)}) %all-gather.9.cloned.1.call-update) | async-done | bytes 1048592 | tf_op jit(solution)/shard_map/all_gather | solution.py:55
  76.9 2.6 reshape.88
  79.5 2.7 copy.33
  82.3 23.6 %all-gather.11.cloned.1.call-done = bf16[2048,2,128]{0,2,1:T(8,128)(2,1)} async-done(((bf16[512,2,128]{0,2,1:T(8,128)(2,1)}), bf16[2048,2,128]{0,2,1:T(8,128)(2,1)}) %all-gather.11.cloned.1.call-update) | async-done | bytes 1048592 | tf_op jit(solution)/shard_map/all_gather | solution.py:56
  105.9 3.7 copy.32
  109.5 32.0 %while.37 = (s32[]{:T(128)}, f32[2,512]{1,0:T(2,128)S(1)}, f32[512,2,128]{0,2,1:T(8,128)}, bf16[4,512,2,128]{3,1,2,0:T(8,128)(2,1)}, bf16[512,2,128]{2,0,1:T(8,1...) while((s32[]{:T(128)}, f32[2,512]{1,0:T(2,128)S(1)}, ...), condition=%wide.region_6.7_spmd.clone, body=%wide.region_4.6_spmd.clone.sunk | while | flops 271844352 | bytes 8143544 | solution.py:75
  109.5 2.8 bitcast_reduce_fusion.2
  114.3 3.2 fusion.103
  117.5 2.8 bitcast_reduce_fusion.2
  122.3 3.2 fusion.103
  125.5 2.8 bitcast_reduce_fusion.2
  130.3 3.2 fusion.103
  133.5 2.8 bitcast_reduce_fusion.2
  138.3 3.2 fusion.103
  141.5 3.5 multiply_reduce_fusion.3
  145.1 1.9 copy.37
  147.0 1.8 copy.41
  148.8 2.4 copy.76
  151.2 33.2 %while.38 = (s32[]{:T(128)}, f32[512,2,128]{0,2,1:T(8,128)}, bf16[4,512,2,128]{1,3,2,0:T(8,128)(2,1)}, bf16[512,2,128]{2,1,0:T(2,128)(2,1)S(1)}, f32[2]{0:T(128)...) while((s32[]{:T(128)}, f32[512,2,128]{0,2,1:T(8,128)}, ...), condition=%wide.region_10.11_spmd.clone, body=%wide.region_9.10_spmd.clone.sunk | while | flops 406585344 | bytes 7087251 | solution.py:131
  151.2 2.8 fusion.109
  154.0 1.8 dynamic-slice_bitcast_fusion.5
  155.9 3.6 fusion.110
  159.5 2.8 fusion.109
  162.3 1.8 dynamic-slice_bitcast_fusion.5
  164.1 3.6 fusion.110
  167.8 2.8 fusion.109
  170.6 1.8 dynamic-slice_bitcast_fusion.5
  172.4 3.8 fusion.110
  176.2 2.8 fusion.109
  179.0 1.8 dynamic-slice_bitcast_fusion.5
  180.8 3.6 fusion.110
  184.4 2.0 copy.39
  190.8 13.2 %all_gather.33 = f32[2048,2]{0,1:T(2,128)S(1)} all-gather(f32[512,2]{0,1:T(2,128)S(1)} %get-tuple-element.734), channel_id=1, replica_groups=mesh['row'=4,'col'=8] {'row'}, dimensions={0}, use_global_device_ids=true | all-gather | bytes 20480 | tf_op jit(solution)/shard_map/all_gather | solution.py:137
  204.0 13.2 %all_gather.31 = f32[2048,2]{0,1:T(2,128)S(1)} all-gather(f32[512,2]{0,1:T(2,128)S(1)} %fusion.81), channel_id=1, replica_groups=mesh['row'=4,'col'=8] {'row'}, dimensions={0}, use_global_device_ids=true | all-gather | bytes 20480 | tf_op jit(solution)/shard_map/all_gather | solution.py:136
  217.2 3.4 convolution_convert_fusion.2
  220.9 36.4 %while.39 = (s32[]{:T(128)}, f32[512,2,128]{0,2,1:T(8,128)}, f32[512,2,128]{0,2,1:T(8,128)}, bf16[4,512,2,128]{3,1,0,2:T(8,128)(2,1)}, bf16[512,2,128]{2,0,1:T(8...) while((s32[]{:T(128)}, f32[512,2,128]{0,2,1:T(8,128)}, ...), condition=%wide.region_13.14_spmd.clone, body=%wide.region_12.13_spmd.clone.sunk | while | flops 541589504 | bytes 9988260 | solution.py:161
  221.0 2.9 exponential_multiply_fusion.3
  223.9 2.8 fusion.119
  226.7 3.2 fusion.118
  230.0 2.9 exponential_multiply_fusion.3
  232.8 2.9 fusion.119
  235.8 3.3 fusion.118
  239.1 2.9 exponential_multiply_fusion.3
  242.0 2.9 fusion.119
  244.9 3.3 fusion.118
  248.2 2.9 exponential_multiply_fusion.3
  251.1 2.9 fusion.119
  254.0 3.3 fusion.118
  262.7 4.3 %bitcast_convert_fusion.2 = bf16[512,2048]{1,0:T(8,128)(2,1)} fusion(bf16[3,2048,256]{2,1,0:T(8,128)(2,1)S(1)} %copy-done, bf16[1,512,256]{2,1,0:T(8,128)(2,1)} %copy.59, bf16[1,512,256]{2,1,0:T(8,128)(2,1)} %copy.58, bf16[1,512,256]{2,1,0:T(8,128)(2,1)} %stack_reshape.9), kind=kOutput, calls=%fused_computation.57 | convolution fusion | flops 1612447744 | bytes 6029312 | tf_op jit(solution)/shard_map/ksh,kdh->sd/dot_general | solution.py:184
  268.0 5.2 %fusion.50 = bf16[3,2048,256]{1,2,0:T(8,128)(2,1)} fusion(bf16[512,2048]{1,0:T(8,128)(2,1)} %all-gather.7.cloned.1.call-done, bf16[1,512,256]{2,1,0:T(8,128)(2,1)} %copy.59, bf16[1,512,256]{2,1,0:T(8,128)(2,1)} %copy.58, bf16[1,512,256]{2,1,0:T(8,128)(2,1)S(1)} %copy-done.11), kind=kOutput, calls=%fused_computation.60 | convolution fusion | flops 1612972032 | bytes 6029312 | tf_op jit(solution)/shard_map/sd,ksh->kdh/dot_general | solution.py:178
  274.2 3.4 convolution_convert_fusion.1
  277.6 1.8 convert_element_type.101
  279.5 28.2 %reduce-scatter.7.cloned.1.call-done = bf16[64,2048]{1,0:T(8,128)(2,1)} async-done(((bf16[512,2048]{1,0:T(8,128)(2,1)}), bf16[64,2048]{1,0:T(8,128)(2,1)}) %reduce-scatter.7.cloned.1.call-update) | async-done | bytes 262160 | tf_op jit(solution)/shard_map/reduce_scatter | solution.py:183
  308.9 1.8 fusion.64
  310.8 59.7 %reduce-scatter.9.cloned.1.call-done = bf16[3,512,256]{1,2,0:T(8,128)(2,1)} async-done(((bf16[3,2048,256]{1,2,0:T(8,128)(2,1)}), bf16[3,512,256]{1,2,0:T(8,128)(2,1)}) %reduce-scatter.9.cloned.1.call-update) | async-done | bytes 786448 | tf_op jit(solution)/shard_map/reduce_scatter | solution.py:179
  370.5 2.5 copy.49
  373.0 42.2 %reduce-scatter.5.cloned.1.call-done = bf16[64,2048]{1,0:T(8,128)(2,1)} async-done(((bf16[512,2048]{1,0:T(8,128)(2,1)}), bf16[64,2048]{1,0:T(8,128)(2,1)}) %reduce-scatter.5.cloned.1.call-update) | async-done | bytes 262160 | tf_op jit(solution)/shard_map/reduce_scatter | solution.py:82
  (107 shorter events, 30.1 us)
Async XLA Ops:
  7.2 34.6 %copy-start = (bf16[3,2048,256]{2,1,0:T(8,128)(2,1)S(1)}, bf16[3,2048,256]{2,1,0:T(8,128)(2,1)}, u32[]{:S(2)}) copy-start(bf16[3,2048,256]{2,1,0:T(8,128)(2,1)} %param.16) | copy-start | bytes 9437188
  7.2 2.9 copy-start.7
  7.2 34.5 %all-gather.7.cloned.1.call-start = ((), (), s32[]{:S(2)}) async-start(), calls=%async_computation.4 | async-start | bytes 2359296 | tf_op jit(solution)/shard_map/all_gather | solution.py:43
  11.1 65.8 %all-gather.9.cloned.1.call-start = ((), (), s32[]{:S(2)}) async-start(), calls=%async_computation.5 | async-start | bytes 1310720 | tf_op jit(solution)/shard_map/all_gather | solution.py:55
  45.2 1.1 copy-start.10
  46.3 5.0 %copy-start.12 = (f32[2]{0:T(128)S(1)}, f32[2]{0:T(128)}, u32[]{:S(2)}) copy-start(f32[2]{0:T(128)} %param.17) | copy-start | bytes 28
  47.2 0.8 copy-start.4
  48.8 57.1 %all-gather.11.cloned.1.call-start = ((), (), s32[]{:S(2)}) async-start(), calls=%async_computation.6 | async-start | bytes 1310720 | tf_op jit(solution)/shard_map/all_gather | solution.py:56
  50.6 90.9 %all-gather.13.cloned.1.call-start = ((), (), s32[]{:S(2)}) async-start(), calls=%async_computation.8 | async-start | bytes 2359296 | tf_op jit(solution)/shard_map/all_gather | solution.py:88
  51.2 169.7 %all-gather.15.cloned.1.call-start = ((), (), s32[]{:S(2)}) async-start(), calls=%async_computation.9 | async-start | bytes 1310720 | tf_op jit(solution)/shard_map/all_gather | solution.py:140
  59.4 1.0 copy-start.1
  60.4 160.5 %all-gather.17.cloned.1.call-start = ((), (), s32[]{:S(2)}) async-start(), calls=%async_computation.10 | async-start | bytes 1310720 | tf_op jit(solution)/shard_map/all_gather | solution.py:141
  79.5 30.0 %copy-start.2 = (bf16[512,2,128]{2,0,1:T(8,128)(2,1)S(1)}, bf16[512,2,128]{2,0,1:T(8,128)(2,1)}, u32[]{:S(2)}) copy-start(bf16[512,2,128]{2,0,1:T(8,128)(2,1)} %copy-done.1) | copy-start | bytes 786436
  114.3 3.2 copy-start.3
  122.3 3.2 copy-start.3
  130.3 3.2 copy-start.3
  138.3 3.2 copy-start.3
  145.1 6.1 %copy-start.6 = (bf16[512,2,128]{2,1,0:T(2,128)(2,1)S(1)}, bf16[512,2,128]{2,1,0:T(2,128)(2,1)}, u32[]{:S(2)}) copy-start(bf16[512,2,128]{2,1,0:T(2,128)(2,1)} %copy.36) | copy-start | bytes 786436
  151.2 126.4 %reduce-scatter.11.cloned.1.call-start = ((), (), s32[]{:S(2)}) async-start(), calls=%async_computation.13 | async-start | bytes 1310720 | tf_op jit(solution)/shard_map/reduce_scatter | solution.py:92
  217.2 3.7 copy-start.5
  220.7 87.1 %reduce-scatter.7.cloned.1.call-start = ((), (), s32[]{:S(2)}) async-start(), calls=%async_computation.11 | async-start | bytes 2359296 | tf_op jit(solution)/shard_map/reduce_scatter | solution.py:183
  267.0 0.9 copy-start.11
  267.1 103.4 %reduce-scatter.9.cloned.1.call-start = ((), (), s32[]{:S(2)}) async-start(), calls=%async_computation.12 | async-start | bytes 3932160 | tf_op jit(solution)/shard_map/reduce_scatter | solution.py:179
  273.2 1.0 copy-start.9
  273.3 142.0 %reduce-scatter.5.cloned.1.call-start = ((), (), s32[]{:S(2)}) async-start(), calls=%async_computation.7 | async-start | bytes 2359296 | tf_op jit(solution)/shard_map/reduce_scatter | solution.py:82
  277.6 30.2 %copy-start.8 = (bf16[64,2048]{1,0:T(8,128)(2,1)S(1)}, bf16[64,2048]{1,0:T(8,128)(2,1)}, u32[]{:S(2)}) copy-start(bf16[64,2048]{1,0:T(8,128)(2,1)} %param.13) | copy-start | bytes 786436
Sparse Core Ops, SparseCore 0:
  11.2 30.4 all-gather.6
  48.9 27.9 all-gather.8
  78.5 27.3 all-gather.10
  107.6 27.1 all-gather.12
  136.8 28.0 all-gather.14
  166.3 27.3 all-gather.16
  220.8 26.5 reduce-scatter.10
  267.2 40.4 reduce-scatter.6
  310.0 60.3 reduce-scatter.8
  374.2 41.0 reduce-scatter.4
where the time goes:
time: 424 us; the launch traced here: 422 us
  waiting for transfers between devices  202 us (48%)
  matrix products  109 us (26%)
  local copies, waits for them, and re-layouts  50.9 us (12%)
  blocking collectives  26.4 us (6%)
  other arithmetic  17.9 us (4%)
  between operations  15.3 us (4%)
    reduce_scatter x1, waiting for transfers between devices, per_device(): lax.psum_scatter(qkv_part.astype(jnp.bfloat16), 'row', scatter_dimension=...  59.7 us
    reduce_scatter x1, waiting for transfers between devices, per_device(): lax.psum_scatter(jnp.dot(rows, out_weight, preferred_element_type=jnp.flo...  42.2 us
    all_gather x1, waiting for transfers between devices, per_device(): group = lax.all_gather(hidden, 'col', axis=0, tiled=True)  30.6 us
    reduce_scatter x1, waiting for transfers between devices, per_device(): lax.psum_scatter(jnp.einsum('ksh,kdh->sd', rows, qkv_weight, preferred_el...  28.2 us
    all_gather x1, waiting for transfers between devices, per_device(): value_piece = lax.all_gather(value_heads, 'row', axis=0, tiled=True)  23.6 us
    dot_general x8, matrix products, pair_terms(): jnp.einsum('qhd,khd->hqk', query_rows, key_block, preferred_element_type=...  22.8 us
    all_gather x1, waiting for transfers between devices, per_device(): key_piece = lax.all_gather(key_heads, 'row', axis=0, tiled=True)  16.5 us
    unnamed x30, local copies, waits for them, and re-layouts  15.4 us
  transfers between devices with their start and end apart: 10, of which 6 were waited for; matrix products, arithmetic and copies ran while one was open for 39% of the time, Pallas kernels for 0%

commit v1 on v0

--- a/solution.py
+++ b/solution.py
@@ -53,7 +53,15 @@
     )
     carry = start_state
     key_piece = lax.all_gather(key_heads, "row", axis=0, tiled=True)
-    value_piece = lax.all_gather(value_heads, "row", axis=0, tiled=True)
+    history = [value_heads]
+    axis_n = lax.axis_size("row")
+    for hop_no in range(axis_n - 1):
+        history.append(
+            lax.ppermute(history[-1], "row", [(k, (k + 1) % axis_n) for k in range(axis_n)])
+        )
+    value_piece = jnp.roll(
+        jnp.concatenate(history[::-1], 0), (lax.axis_index("row") + 1) * value_heads.shape[0], 0
+    )
     size = math.gcd(key_piece.shape[0], 512)
 
     def attend_step(state, block):

time: 424 us -> 420 us (level)
  waiting for transfers between devices: 202 us -> 194 us
  starting transfers between devices: 0.59 us -> 4.88 us
    ppermute x0 -> x3, waiting for transfers between devices: none -> 29.1 us  [per_device(): lax.ppermute(history[-1], 'row', [(k, (k + 1) % axis_n) for k in range(ax...]
    all_gather x1, waiting for transfers between devices: 23.6 us -> 3.61 us  [per_device(): value_piece = lax.all_gather(value_heads, 'row', axis=0, tiled=True)]
    all_gather x1, waiting for transfers between devices: 16.5 us -> 0.01 us  [per_device(): key_piece = lax.all_gather(key_heads, 'row', axis=0, tiled=True)]
    dynamic_slice x8 -> x1, local copies, waits for them, and re-layouts: 8 us -> 1.05 us  [per_device(): jnp.roll(jnp.concatenate(history[::-1], 0), (lax.axis_index('row') + 1) *...]
    unnamed x30 -> x41, local copies, waits for them, and re-layouts: 15.4 us -> 20.3 us
    ppermute x0 -> x3, starting transfers between devices: none -> 4.29 us  [per_device(): lax.ppermute(history[-1], 'row', [(k, (k + 1) % axis_n) for k in range(ax...]
  transfers between devices with their start and end apart: 10 -> 13, of which waited for: 6 -> 8; matrix products, arithmetic and copies ran while one was open for 39% -> 39% of each run, Pallas kernels for 0% -> 0%
where the time goes in v1:
time: 420 us; the launch traced here: 418 us
  waiting for transfers between devices  194 us (46%)
  matrix products  109 us (26%)
  local copies, waits for them, and re-layouts  49.8 us (12%)
  blocking collectives  26.7 us (6%)
  other arithmetic  17.9 us (4%)
  between operations  15.2 us (4%)
  starting transfers between devices  4.88 us (1%)
    reduce_scatter x1, waiting for transfers between devices, per_device(): lax.psum_scatter(qkv_part.astype(jnp.bfloat16), 'row', scatter_dimension=...  59.7 us
    reduce_scatter x1, waiting for transfers between devices, per_device(): lax.psum_scatter(jnp.dot(rows, out_weight, preferred_element_type=jnp.flo...  42.2 us
    all_gather x1, waiting for transfers between devices, per_device(): group = lax.all_gather(hidden, 'col', axis=0, tiled=True)  30.6 us
    ppermute x3, waiting for transfers between devices, per_device(): lax.ppermute(history[-1], 'row', [(k, (k + 1) % axis_n) for k in range(ax...  29.1 us
    reduce_scatter x1, waiting for transfers between devices, per_device(): lax.psum_scatter(jnp.einsum('ksh,kdh->sd', rows, qkv_weight, preferred_el...  28.3 us
    dot_general x8, matrix products, pair_terms(): jnp.einsum('qhd,khd->hqk', query_rows, key_block, preferred_element_type=...  22.7 us
    unnamed x41, local copies, waits for them, and re-layouts  20.3 us
    dot_general x4, matrix products, query_step(): jnp.einsum('hqk,khd->qhd', dscores, key_block, preferred_element_type=jnp...  14.6 us
  transfers between devices with their start and end apart: 13, of which 8 were waited for; matrix products, arithmetic and copies ran while one was open for 39% of the time, Pallas kernels for 0%

profile of v1, /device:TPU:0, one launch (start us, length us, event | category | flops | bytes accessed | tf_op | source)
XLA Modules:
  0.0 418.0 jit_solution(6942737748760502146)
XLA Ops:
  8.1 1.9 multiply_reduce_fusion
  11.1 30.6 %all-gather.7.cloned.1.call-done = bf16[512,2048]{1,0:T(8,128)(2,1)} async-done(((bf16[64,2048]{1,0:T(8,128)(2,1)}), bf16[512,2048]{1,0:T(8,128)(2,1)}) %all-gather.7.cloned.1.call-update) | async-done | bytes 2097168 | tf_op jit(solution)/shard_map/all_gather | solution.py:43
  41.7 3.4 fusion.56
  49.6 1.8 slice.17
  51.4 1.8 copy.31
  54.8 12.6 %collective-permute-done = bf16[512,2,128]{2,0,1:T(8,128)(2,1)} collective-permute-done((bf16[512,2,128]{2,0,1:T(8,128)(2,1)}, bf16[512,2,128]{2,0,1:T(8,128)(2,1)}, u32[]{:S(2)}, u32[]{:S(2)}) %collective-permute-start) | collective-permute-done | bytes 262176 | tf_op jit(solution)/shard_map/ppermute | solution.py:60
  67.4 2.8 collective-permute-start.1
  71.3 15.1 %collective-permute-done.1 = bf16[512,2,128]{2,0,1:T(8,128)(2,1)} collective-permute-done((bf16[512,2,128]{2,0,1:T(8,128)(2,1)}, bf16[512,2,128]{2,0,1:T(8,128)(2,1)}, u32[]{:S(2)}, u32[]{:S(2)}) %collective-permute-start.1) | collective-permute-done | bytes 262176 | tf_op jit(solution)/shard_map/ppermute | solution.py:60
  86.4 2.1 copy.30
  88.5 1.8 copy.45
  102.9 2.7 reshape.90
  105.6 2.7 copy.34
  108.2 23.6 %while.37 = (s32[]{:T(128)}, f32[2,512]{1,0:T(2,128)S(1)}, f32[512,2,128]{0,2,1:T(8,128)}, bf16[4,512,2,128]{3,1,2,0:T(8,128)(2,1)}, bf16[512,2,128]{2,0,1:T(8,1...) while((s32[]{:T(128)}, f32[2,512]{1,0:T(2,128)S(1)}, ...), condition=%wide.region_6.7_spmd.clone, body=%wide.region_4.6_spmd.clone.sunk | while | flops 271844352 | bytes 6046864 | solution.py:83
  108.2 2.7 bitcast_reduce_fusion.2
  111.0 3.1 fusion.105
  114.1 2.7 bitcast_reduce_fusion.2
  116.8 3.1 fusion.105
  120.0 2.7 bitcast_reduce_fusion.2
  122.7 3.2 fusion.105
  125.9 2.7 bitcast_reduce_fusion.2
  128.6 3.1 fusion.105
  131.8 3.4 multiply_reduce_fusion.3
  137.0 2.3 copy.78
  139.4 3.6 all-gather.11.cloned.1.call-done
  143.0 3.7 copy.36
  146.7 33.2 %while.38 = (s32[]{:T(128)}, f32[512,2,128]{0,2,1:T(8,128)}, bf16[4,512,2,128]{1,3,2,0:T(8,128)(2,1)}, bf16[512,2,128]{2,1,0:T(2,128)(2,1)S(1)}, f32[2]{0:T(128)...) while((s32[]{:T(128)}, f32[512,2,128]{0,2,1:T(8,128)}, ...), condition=%wide.region_10.11_spmd.clone, body=%wide.region_9.10_spmd.clone.sunk | while | flops 406585344 | bytes 7087251 | solution.py:139
  146.7 2.8 fusion.111
  149.5 1.8 dynamic-slice_bitcast_fusion.5
  151.3 3.7 fusion.112
  155.0 2.8 fusion.111
  157.8 1.8 dynamic-slice_bitcast_fusion.5
  159.7 3.7 fusion.112
  163.3 2.8 fusion.111
  166.1 1.8 dynamic-slice_bitcast_fusion.5
  168.0 3.6 fusion.112
  171.6 2.8 fusion.111
  174.4 1.8 dynamic-slice_bitcast_fusion.5
  176.2 3.6 fusion.112
  179.9 2.1 copy.41
  186.2 13.5 %all_gather.32 = f32[2048,2]{0,1:T(2,128)S(1)} all-gather(f32[512,2]{0,1:T(2,128)S(1)} %get-tuple-element.726), channel_id=1, replica_groups=mesh['row'=4,'col'=8] {'row'}, dimensions={0}, use_global_device_ids=true | all-gather | bytes 20480 | tf_op jit(solution)/shard_map/all_gather | solution.py:145
  199.7 13.2 %all_gather.30 = f32[2048,2]{0,1:T(2,128)S(1)} all-gather(f32[512,2]{0,1:T(2,128)S(1)} %fusion.83), channel_id=1, replica_groups=mesh['row'=4,'col'=8] {'row'}, dimensions={0}, use_global_device_ids=true | all-gather | bytes 20480 | tf_op jit(solution)/shard_map/all_gather | solution.py:144
  212.9 3.4 convolution_convert_fusion.2
  216.7 36.4 %while.39 = (s32[]{:T(128)}, f32[512,2,128]{0,2,1:T(8,128)}, f32[512,2,128]{0,2,1:T(8,128)}, bf16[4,512,2,128]{3,1,0,2:T(8,128)(2,1)}, bf16[512,2,128]{2,0,1:T(8...) while((s32[]{:T(128)}, f32[512,2,128]{0,2,1:T(8,128)}, ...), condition=%wide.region_13.14_spmd.clone, body=%wide.region_12.13_spmd.clone.sunk | while | flops 541589504 | bytes 9988260 | solution.py:169
  216.7 2.9 exponential_multiply_fusion.3
  219.6 2.9 fusion.121
  222.5 3.2 fusion.120
  225.7 2.9 exponential_multiply_fusion.3
  228.6 3.0 fusion.121
  231.5 3.3 fusion.120
  234.8 2.9 exponential_multiply_fusion.3
  237.7 3.0 fusion.121
  240.7 3.3 fusion.120
  244.0 2.9 exponential_multiply_fusion.3
  246.9 2.9 fusion.121
  249.8 3.3 fusion.120
  258.5 4.3 %bitcast_convert_fusion.2 = bf16[512,2048]{1,0:T(8,128)(2,1)} fusion(bf16[3,2048,256]{2,1,0:T(8,128)(2,1)S(1)} %copy-done, bf16[1,512,256]{2,1,0:T(8,128)(2,1)} %copy.61, bf16[1,512,256]{2,1,0:T(8,128)(2,1)} %copy.60, bf16[1,512,256]{2,1,0:T(8,128)(2,1)} %stack_reshape.9), kind=kOutput, calls=%fused_computation.58 | convolution fusion | flops 1612447744 | bytes 6029312 | tf_op jit(solution)/shard_map/ksh,kdh->sd/dot_general | solution.py:192
  263.8 5.3 %fusion.52 = bf16[3,2048,256]{1,2,0:T(8,128)(2,1)} fusion(bf16[512,2048]{1,0:T(8,128)(2,1)} %all-gather.7.cloned.1.call-done, bf16[1,512,256]{2,1,0:T(8,128)(2,1)} %copy.61, bf16[1,512,256]{2,1,0:T(8,128)(2,1)} %copy.60, bf16[1,512,256]{2,1,0:T(8,128)(2,1)S(1)} %copy-done.12), kind=kOutput, calls=%fused_computation.61 | convolution fusion | flops 1612972032 | bytes 6029312 | tf_op jit(solution)/shard_map/sd,ksh->kdh/dot_general | solution.py:186
  270.0 3.4 convolution_convert_fusion.1
  273.5 1.8 convert_element_type.101
  275.3 28.3 %reduce-scatter.7.cloned.1.call-done = bf16[64,2048]{1,0:T(8,128)(2,1)} async-done(((bf16[512,2048]{1,0:T(8,128)(2,1)}), bf16[64,2048]{1,0:T(8,128)(2,1)}) %reduce-scatter.7.cloned.1.call-update) | async-done | bytes 262160 | tf_op jit(solution)/shard_map/reduce_scatter | solution.py:191
  304.9 1.8 fusion.66
  306.7 59.7 %reduce-scatter.9.cloned.1.call-done = bf16[3,512,256]{1,2,0:T(8,128)(2,1)} async-done(((bf16[3,2048,256]{1,2,0:T(8,128)(2,1)}), bf16[3,512,256]{1,2,0:T(8,128)(2,1)}) %reduce-scatter.9.cloned.1.call-update) | async-done | bytes 786448 | tf_op jit(solution)/shard_map/reduce_scatter | solution.py:187
  366.4 2.5 copy.51
  368.9 42.2 %reduce-scatter.5.cloned.1.call-done = bf16[64,2048]{1,0:T(8,128)(2,1)} async-done(((bf16[512,2048]{1,0:T(8,128)(2,1)}), bf16[64,2048]{1,0:T(8,128)(2,1)}) %reduce-scatter.5.cloned.1.call-update) | async-done | bytes 262160 | tf_op jit(solution)/shard_map/reduce_scatter | solution.py:90
  (111 shorter events, 35.7 us)
Async XLA Ops:
  7.2 34.6 %copy-start = (bf16[3,2048,256]{2,1,0:T(8,128)(2,1)S(1)}, bf16[3,2048,256]{2,1,0:T(8,128)(2,1)}, u32[]{:S(2)}) copy-start(bf16[3,2048,256]{2,1,0:T(8,128)(2,1)} %param.16) | copy-start | bytes 9437188
  7.2 2.9 copy-start.6
  7.2 34.5 %all-gather.7.cloned.1.call-start = ((), (), s32[]{:S(2)}) async-start(), calls=%async_computation.4 | async-start | bytes 2359296 | tf_op jit(solution)/shard_map/all_gather | solution.py:43
  11.1 91.8 %all-gather.9.cloned.1.call-start = ((), (), s32[]{:S(2)}) async-start(), calls=%async_computation.5 | async-start | bytes 1310720 | tf_op jit(solution)/shard_map/all_gather | solution.py:55
  45.2 1.1 copy-start.11
  47.2 0.8 copy-start.3
  47.2 23.0 %copy-start.13 = (f32[2]{0:T(128)S(1)}, f32[2]{0:T(128)}, u32[]{:S(2)}) copy-start(f32[2]{0:T(128)} %param.17) | copy-start | bytes 28
  48.8 83.0 %all-gather.13.cloned.1.call-start = ((), (), s32[]{:S(2)}) async-start(), calls=%async_computation.8 | async-start | bytes 2359296 | tf_op jit(solution)/shard_map/all_gather | solution.py:96
  49.5 93.5 %all-gather.11.cloned.1.call-start = ((), (), s32[]{:S(2)}) async-start(), calls=%async_computation.7 | async-start | bytes 1310720 | tf_op jit(solution)/shard_map/all_gather | solution.py:127
  51.4 38.9 %copy-start.8 = (bf16[1,512,256]{1,2,0:T(8,128)(2,1)S(1)}, bf16[1,512,256]{1,2,0:T(8,128)(2,1)}, u32[]{:S(2)}) copy-start(bf16[1,512,256]{1,2,0:T(8,128)(2,1)} %slice.17) | copy-start | bytes 786436
  51.4 165.2 %all-gather.15.cloned.1.call-start = ((), (), s32[]{:S(2)}) async-start(), calls=%async_computation.9 | async-start | bytes 1310720 | tf_op jit(solution)/shard_map/all_gather | solution.py:148
  53.3 14.1 %collective-permute-start = (bf16[512,2,128]{2,0,1:T(8,128)(2,1)}, bf16[512,2,128]{2,0,1:T(8,128)(2,1)}, u32[]{:S(2)}, u32[]{:S(2)}) collective-permute-start(bf16[512,2,128]{2,0,1:T(8,128)(2,1)} %copy.31), channel_id=1, source_target_pairs={{0,8},{8,16},{16,24},{24,0},{1,9},{9,17},{17,25},{25,1},{2,10},{10... | collective-permute-start | bytes 786440 | tf_op jit(solution)/shard_map/ppermute | solution.py:60
  67.4 19.0 %collective-permute-start.1 = (bf16[512,2,128]{2,0,1:T(8,128)(2,1)}, bf16[512,2,128]{2,0,1:T(8,128)(2,1)}, u32[]{:S(2)}, u32[]{:S(2)}) collective-permute-start(bf16[512,2,128]{2,0,1:T(8,128)(2,1)} %collective-permute-done), channel_id=1, source_target_pairs={{0,8},{8,16},{16,24},{24,0},{1,9},{9,17},{17,25},{25,1},{2,10},{10... | collective-permute-start | bytes 786440 | tf_op jit(solution)/shard_map/ppermute | solution.py:60
  86.4 8.5 %collective-permute-start.2 = (bf16[512,2,128]{2,0,1:T(8,128)(2,1)}, bf16[512,2,128]{2,0,1:T(8,128)(2,1)}, u32[]{:S(2)}, u32[]{:S(2)}) collective-permute-start(bf16[512,2,128]{2,0,1:T(8,128)(2,1)} %collective-permute-done.1), channel_id=1, source_target_pairs={{0,8},{8,16},{16,24},{24,0},{1,9},{9,17},{17,25},{25,1},{2,10},{10... | collective-permute-start | bytes 786440 | tf_op jit(solution)/shard_map/ppermute | solution.py:60
  92.4 1.0 copy-start.1
  93.4 8.4 %copy-start.10 = (bf16[512,2,128]{2,0,1:T(8,128)(2,1)S(1)}, bf16[512,2,128]{2,0,1:T(8,128)(2,1)}, u32[]{:S(2)}) copy-start(bf16[512,2,128]{2,0,1:T(8,128)(2,1)} %copy.31) | copy-start | bytes 786436
  93.4 123.2 %all-gather.17.cloned.1.call-start = ((), (), s32[]{:S(2)}) async-start(), calls=%async_computation.10 | async-start | bytes 1310720 | tf_op jit(solution)/shard_map/all_gather | solution.py:149
  102.9 5.3 %copy-start.2 = (bf16[512,2,128]{2,0,1:T(8,128)(2,1)S(1)}, bf16[512,2,128]{2,0,1:T(8,128)(2,1)}, u32[]{:S(2)}) copy-start(bf16[512,2,128]{2,0,1:T(8,128)(2,1)} %copy-done.1) | copy-start | bytes 786436
  137.0 9.7 %copy-start.5 = (bf16[512,2,128]{2,1,0:T(2,128)(2,1)S(1)}, bf16[512,2,128]{2,1,0:T(2,128)(2,1)}, u32[]{:S(2)}) copy-start(bf16[512,2,128]{2,1,0:T(2,128)(2,1)} %copy.38) | copy-start | bytes 786436
  139.3 134.1 %reduce-scatter.11.cloned.1.call-start = ((), (), s32[]{:S(2)}) async-start(), calls=%async_computation.13 | async-start | bytes 1310720 | tf_op jit(solution)/shard_map/reduce_scatter | solution.py:100
  212.9 3.7 copy-start.4
  216.4 87.3 %reduce-scatter.7.cloned.1.call-start = ((), (), s32[]{:S(2)}) async-start(), calls=%async_computation.11 | async-start | bytes 2359296 | tf_op jit(solution)/shard_map/reduce_scatter | solution.py:191
  262.8 0.9 copy-start.12
  262.8 103.5 %reduce-scatter.9.cloned.1.call-start = ((), (), s32[]{:S(2)}) async-start(), calls=%async_computation.12 | async-start | bytes 3932160 | tf_op jit(solution)/shard_map/reduce_scatter | solution.py:187
  269.0 1.0 copy-start.9
  269.1 142.1 %reduce-scatter.5.cloned.1.call-start = ((), (), s32[]{:S(2)}) async-start(), calls=%async_computation.6 | async-start | bytes 2359296 | tf_op jit(solution)/shard_map/reduce_scatter | solution.py:90
  273.4 30.2 %copy-start.7 = (bf16[64,2048]{1,0:T(8,128)(2,1)S(1)}, bf16[64,2048]{1,0:T(8,128)(2,1)}, u32[]{:S(2)}) copy-start(bf16[64,2048]{1,0:T(8,128)(2,1)} %param.13) | copy-start | bytes 786436
Sparse Core Ops, SparseCore 0:
  11.2 30.4 all-gather.6
  48.9 37.5 all-gather.8
  88.4 25.0 all-gather.12
  115.0 27.9 all-gather.10
  145.0 27.3 all-gather.14
  173.8 27.6 all-gather.16
  216.5 26.6 reduce-scatter.10
  263.0 40.6 reduce-scatter.6
  306.0 60.3 reduce-scatter.8
  370.1 41.0 reduce-scatter.4
